TPU v7x, 256 devices: a whole 4x4x8 slice. The times are simulated.
256 devices in a mesh: dp: 128 (over z, x, y_hi, core), tensor: 2 (over y_lo).
Axes of the slice: x: 4, y: 4 (y_hi: 2, y_lo: 2; y = y_hi * 2 + y_lo), z: 8, core: 2. Of those that a mesh axis runs over, the one named last changes fastest.
Arguments:
- tokens: bfloat16 [16384, 2048], P('dp'), may hold values from -16 to 16
- teacher: bfloat16 [16384, 2048], P('dp'), may hold values from -6 to 6
- inner_weight: float32 [2048, 512], P('dp', 'tensor'), may hold values from -0.125 to 0.125
- output_weight: bfloat16 [2048, 2048], P('dp', 'tensor'), may hold values from -0.125 to 0.125
- inner_first: float32 [2048, 512], P('dp', 'tensor'), may hold values from -2 to 2
- inner_second: float32 [2048, 512], P('dp', 'tensor'), may hold values from 0.2 to 2
- state_weight: bfloat16 [2048, 32], replicated, may hold values from -0.03125 to 0.03125
- step_weight: bfloat16 [2048, 16], P(None, 'tensor'), may hold values from -0.0390625 to 0.0390625
- step_bias: float32 [16], P('tensor'), may hold values from -4 to 0
- decay_log: float32 [16], P('tensor'), may hold values from -3 to 1
- skip_gain: float32 [16], P('tensor'), may hold values from 0.5 to 1.5
Outputs:
- distill_loss: float32 [], replicated
- inner_update: float32 [2048, 512], P('dp', 'tensor')
- inner_first_next: float32 [2048, 512], P('dp', 'tensor')
- inner_second_next: float32 [2048, 512], P('dp', 'tensor')
All inputs are finite; a program needn't handle non-finite values.
Results may differ from a plain program's by a relative error of at most 0.0016.
Values may be sent and summed in bfloat16 or wider, within the bound.
A program may use at most 64 MiB of HBM per device.

v0:
```python
import jax
import jax.numpy as jnp
from jax import lax
from jax.sharding import Mesh
from jax.sharding import PartitionSpec as P

HEADS = 16
GROUPS = 4
HEAD_DIM = 128
STEP = 20
DP = ("dp_0", "dp_1", "dp_2", "dp_3")
DP_TENSOR = ("dp_0", "dp_1", "dp_2", "dp_3", "tensor")
beta_one = 0.9
beta_two = 0.95
adam_eps = 1e-08
weight_decay = 0.1
norm_eps = 1e-06


def sent_together(arrays, axis, dim, along):
    widths = [a.shape[along] for a in arrays]
    both = jnp.concatenate(arrays, axis=along)
    whole = lax.all_gather(both, axis, axis=dim, tiled=True)
    return tuple(jnp.split(whole, [sum(widths[:k]) for k in range(1, len(widths))], axis=along))


def sent_to_all(x, axis):
    peers = lax.axis_size(axis)
    return lax.all_to_all(jnp.broadcast_to(x[None], (peers, *x.shape)), axis, 0, 0, tiled=True)


def of_everyone(x, axis):
    everything = sent_to_all(x, axis)
    return jnp.sum(everything, axis=0)


def cut_along(x, dim, peers):
    before, after = (x.shape[:dim], x.shape[dim + 1 :])
    return jnp.moveaxis(x.reshape(*before, peers, -1, *after), dim, 0)


def sum_at_owner(x, axis, dim):
    peers = lax.axis_size(axis)
    pieces = lax.all_to_all(cut_along(x, dim, peers), axis, 0, 0, tiled=True)
    return jnp.sum(pieces, axis=0)


def sum_in_two_steps(x, axes, dim):
    far, near = axes
    own = sum_at_owner(cut_along(x, dim, lax.axis_size(far)), near, dim + 1)
    return jnp.sum(lax.all_to_all(own, far, 0, 0, tiled=True), axis=0)


def one_axis_at_a_time(x, axes):
    for axis in axes:
        x = lax.psum(x, axis)
    return x


def mixing(sequence, state_weight, step_weight, step_bias, decay_log):
    state_width = state_weight.shape[1] // 2
    projected = jnp.dot(sequence, state_weight, preferred_element_type=jnp.float32)
    b_coef = projected[:, :state_width]
    c_coef = projected[:, state_width:]
    gram_matrix = jnp.dot(c_coef, b_coef.T, precision=lax.Precision.HIGHEST)
    step_size = jax.nn.softplus(
        jnp.dot(sequence, step_weight, preferred_element_type=jnp.float32) + step_bias
    )
    rate_step = jnp.exp(decay_log) * step_size
    cumulative = jnp.cumsum(rate_step, axis=0).T
    length = sequence.shape[0]
    row_later = lax.broadcasted_iota(jnp.int32, (length, length), 0)
    earlier = lax.broadcasted_iota(jnp.int32, (length, length), 1)
    causal = row_later >= earlier
    log_decay = cumulative[:, None, :] - cumulative[:, :, None]
    decay_matrix = jnp.where(causal[None], jnp.exp(jnp.minimum(log_decay, 0.0)), 0.0)
    return (gram_matrix[None] * decay_matrix * step_size.T[:, None, :]).astype(jnp.bfloat16)


def contract_rows(left, right):
    return lax.dot_general(
        left, right, (((0,), (0,)), ((), ())), preferred_element_type=jnp.float32
    )


def on_device(
    tokens,
    teacher,
    inner_weight,
    output_weight,
    inner_first,
    inner_second,
    state_weight,
    step_weight,
    step_bias,
    decay_log,
    skip_gain,
):
    seq_rows, model_width = tokens.shape
    heads_here = step_weight.shape[1]
    groups_here = inner_weight.shape[1] // HEAD_DIM
    ratio = HEADS // GROUPS
    total_tokens = seq_rows * lax.axis_size(DP)
    inner_full, output_full = sent_together(
        (inner_weight.astype(jnp.bfloat16), output_weight), DP, 0, 1
    )
    weights_mix = mixing(tokens, state_weight, step_weight, step_bias, decay_log)
    projected = jnp.dot(tokens, inner_full, preferred_element_type=jnp.float32).astype(jnp.bfloat16)
    heads_in = jnp.repeat(projected.reshape(seq_rows, groups_here, HEAD_DIM), ratio, axis=1)
    mixed = jnp.einsum(
        "hts,shp->thp", weights_mix, heads_in, preferred_element_type=jnp.float32
    ) + skip_gain[None, :, None] * heads_in.astype(jnp.float32)
    inner = mixed.astype(jnp.bfloat16).reshape(seq_rows, heads_here * HEAD_DIM)
    partial_out = lax.dot_general(
        inner, output_full, (((1,), (1,)), ((), ())), preferred_element_type=jnp.float32
    )
    student = of_everyone(partial_out, "tensor")
    error_rows = student - teacher.astype(jnp.float32)
    square_sum = jnp.where(lax.axis_index("tensor") == 0, jnp.sum(error_rows * error_rows), 0.0)
    grad_out = error_rows.astype(jnp.bfloat16)
    grad_inner = jnp.dot(grad_out, output_full, preferred_element_type=jnp.float32).astype(
        jnp.bfloat16
    )
    grad_heads = grad_inner.reshape(seq_rows, heads_here, HEAD_DIM)
    back = jnp.einsum(
        "hts,thp->shp", weights_mix, grad_heads, preferred_element_type=jnp.float32
    ) + skip_gain[None, :, None] * grad_heads.astype(jnp.float32)
    grouped = jnp.sum(back.reshape(seq_rows, groups_here, ratio, HEAD_DIM), axis=2)
    grad_projected = grouped.astype(jnp.bfloat16).reshape(seq_rows, groups_here * HEAD_DIM)
    inner_grad = sum_in_two_steps(
        contract_rows(tokens, grad_projected), (("dp_0", "dp_1", "dp_2"), "dp_3"), 0
    )
    local_squares = jnp.sum(inner_grad * inner_grad)
    squares_total, error_total = (
        one_axis_at_a_time(local_squares, DP_TENSOR),
        one_axis_at_a_time(square_sum, DP_TENSOR),
    )
    entry_count = model_width * groups_here * HEAD_DIM * lax.axis_size("tensor")
    root_mean = jnp.sqrt(squares_total / entry_count)
    factor = jnp.minimum(1.0, 1.0 / (root_mean + norm_eps))
    distill_loss = error_total / (total_tokens * model_width)
    first_fix = 1.0 - beta_one**STEP
    second_fix = 1.0 - beta_two**STEP
    clipped = factor * inner_grad
    first_next = beta_one * inner_first + (1.0 - beta_one) * clipped
    second_next = beta_two * inner_second + (1.0 - beta_two) * clipped * clipped
    update = (
        first_next / first_fix / (jnp.sqrt(second_next / second_fix) + adam_eps)
        + weight_decay * inner_weight
    )
    return (distill_loss, update, first_next, second_next)


def solution(mesh):
    finer = Mesh(
        mesh.devices.reshape(8, 4, 2, 2, mesh.shape["tensor"]),
        ("dp_0", "dp_1", "dp_2", "dp_3", "tensor"),
    )
    return jax.shard_map(
        on_device,
        mesh=finer,
        in_specs=(
            P(DP, None),
            P(DP, None),
            P(DP, "tensor"),
            P(DP, "tensor"),
            P(DP, "tensor"),
            P(DP, "tensor"),
            P(),
            P(None, "tensor"),
            P("tensor"),
            P("tensor"),
            P("tensor"),
        ),
        out_specs=(P(), P(DP, "tensor"), P(DP, "tensor"), P(DP, "tensor")),
        check_vma=False,
    )
```

profile of v0, /device:TPU:1, one launch (start us, length us, event | category | flops | bytes accessed | tf_op | source)
XLA Modules:
  0.0 278.1 jit_solution(4933198831317484721)
XLA Ops:
  7.2 0.0 copy-start
  7.2 0.0 all-gather.2.cloned.1.call-start
  7.2 0.8 convert_element_type.37
  8.0 1.4 pad_maximum_fusion
  9.4 0.0 all-gather.2.cloned.1.call-update
  9.4 0.7 exp.13
  10.1 0.0 copy-done
  10.1 1.0 compare_select_fusion
  11.1 0.1 fusion.17
  11.2 0.1 copy.30
  11.3 0.2 reduce_window_sum.11
  11.5 1.2 fusion.25
  12.7 0.3 fusion.14
  13.0 124.1 %all-gather.2.cloned.1.call-done = bf16[2048,1280]{1,0:T(8,128)(2,1)} async-done(((bf16[16,1280]{1,0:T(8,128)(2,1)}), bf16[2048,1280]{1,0:T(8,128)(2,1)}) %all-gather.2.cloned.1.call-update) | async-done | bytes 5242896 | tf_op jit(solution)/shard_map/all_gather | solution.py:23
  137.1 1.7 convolution_convert_fusion
  138.9 1.0 fusion.9
  139.9 3.7 %fusion.2 = f32[128,2048]{1,0:T(8,128)S(1)} fusion(bf16[128,1024]{0,1:T(8,128)(2,1)S(1)} %bitcast.59, bf16[2048,1280]{1,0:T(8,128)(2,1)} %all-gather.2.cloned.1.call-done), kind=kOutput, calls=%fused_computation.2 | convolution fusion | flops 536870912 | bytes 5505024 | tf_op jit(solution)/shard_map/dot_general | solution.py:114
  143.6 0.2 broadcast_in_dim.16
  143.9 0.0 copy-start.1
  143.9 27.3 %all_to_all.15 = f32[2,128,2048]{2,1,0:T(8,128)S(1)} all-to-all(f32[2,128,2048]{2,1,0:T(8,128)S(1)} %broadcast_in_dim.16), channel_id=1, replica_groups=mesh['dp_0'=8,'dp_1'=4,'dp_2'=2,'dp_3'=2,'tensor'=2] {'tensor'}, dimensions={0} | all-to-all | bytes 4194304 | tf_op jit(solution)/shard_map/all_to_all | solution.py:29
  171.2 1.2 reduce_sum.54
  172.5 0.0 copy-done.1
  172.5 0.0 copy-start.5
  172.5 3.2 %fusion.6 = bf16[128,1024]{1,0:T(8,128)(2,1)S(1)} fusion(bf16[2048,1280]{1,0:T(8,128)(2,1)} %all-gather.2.cloned.1.call-done, f32[128,2048]{1,0:T(8,128)} %reduce_sum.54, bf16[128,2048]{1,0:T(8,128)(2,1)S(1)} %copy-done.1), kind=kOutput, calls=%fused_computation.9 | convolution fusion | flops 537788416 | bytes 6029312 | tf_op jit(solution)/shard_map/dot_general | solution.py:121
  175.7 0.2 copy.33
  175.9 0.0 copy-done.5
  175.9 0.4 bitcast_reduce_fusion
  176.3 0.4 convolution_bitcast_fusion
  176.7 1.9 copy.34
  178.6 1.8 copy.35
  180.4 6.2 %all_to_all.16 = f32[2,64,16,256]{3,2,1,0:T(8,128)S(1)} all-to-all(f32[2,64,16,256]{3,2,1,0:T(8,128)S(1)} %copy.35), channel_id=1, replica_groups=mesh['dp_0'=8,'dp_1'=4,'dp_2'=2,'dp_3'=2,'tensor'=2] {'dp_3'}, dimensions={0} | all-to-all | bytes 4194304 | tf_op jit(solution)/shard_map/all_to_all | solution.py:44
  186.6 0.0 copy-start.2
  186.6 0.0 copy-start.3
  186.6 0.0 copy-start.4
  186.6 1.3 reduce_sum.57
  187.8 7.8 %all-to-all-start.2 = ((f32[64,16,256]{2,1,0:T(8,128)}), f32[64,16,256]{2,1,0:T(8,128)S(1)}, u32[]{:S(2)}, u32[]{:S(2)}) async-start(f32[64,16,256]{2,1,0:T(8,128)} %reduce_sum.57), calls=%async_computation.2 | async-start | bytes 2097152 | tf_op jit(solution)/shard_map/all_to_all | solution.py:51
  195.7 2.1 multiply_reduce_fusion
  198.4 25.0 %all-to-all-done.2 = f32[64,16,256]{2,1,0:T(8,128)S(1)} async-done(((f32[64,16,256]{2,1,0:T(8,128)}), f32[64,16,256]{2,1,0:T(8,128)S(1)}, u32[]{:S(2)}, u32[]{:S(2)}) %all-to-all-start.2) | async-done | bytes 1048608 | tf_op jit(solution)/shard_map/all_to_all | solution.py:51
  223.4 0.1 reduce_sum.58
  223.5 0.6 multiply_reduce_fusion.1
  224.1 14.2 %all-reduce = (f32[]{:T(128)}, f32[]{:T(128)}) all-reduce(f32[]{:T(128)S(6)} %select_n.18, f32[]{:T(128)} %multiply_reduce_fusion.1), channel_id=1, replica_groups=mesh['dp_0'=8,'dp_1'=4,'dp_2'=2,'dp_3'=2,'tensor'=2] {'dp_0'}, use_global_device_ids=true, to_apply=%region_3.4 | all-reduce | flops 2 | bytes 16 | tf_op jit(solution)/shard_map/psum | solution.py:56
  238.3 7.5 %all-reduce.1 = (f32[]{:T(128)}, f32[]{:T(128)}) all-reduce(f32[]{:T(128)} %get-tuple-element.4, f32[]{:T(128)} %get-tuple-element.5), channel_id=1, replica_groups=mesh['dp_0'=8,'dp_1'=4,'dp_2'=2,'dp_3'=2,'tensor'=2] {'dp_1'}, use_global_device_ids=true, to_apply=%region_4.5 | all-reduce | flops 2 | bytes 16 | tf_op jit(solution)/shard_map/psum | solution.py:56
  245.8 5.9 %all-reduce.4 = (f32[]{:T(128)}, f32[]{:T(128)}) all-reduce(f32[]{:T(128)} %get-tuple-element.6, f32[]{:T(128)} %get-tuple-element.7), channel_id=1, replica_groups=mesh['dp_0'=8,'dp_1'=4,'dp_2'=2,'dp_3'=2,'tensor'=2] {'dp_2'}, use_global_device_ids=true, to_apply=%region_5.6 | all-reduce | flops 2 | bytes 16 | tf_op jit(solution)/shard_map/psum | solution.py:56
  251.7 11.9 %all-reduce.3 = (f32[]{:T(128)}, f32[]{:T(128)}) all-reduce(f32[]{:T(128)} %get-tuple-element.12, f32[]{:T(128)} %get-tuple-element.13), channel_id=1, replica_groups=mesh['dp_0'=8,'dp_1'=4,'dp_2'=2,'dp_3'=2,'tensor'=2] {'dp_3'}, use_global_device_ids=true, to_apply=%region_6.7 | all-reduce | flops 2 | bytes 16 | tf_op jit(solution)/shard_map/psum | solution.py:56
  263.6 4.4 %all-reduce.2 = (f32[]{:T(128)}, f32[]{:T(128)}) all-reduce(f32[]{:T(128)} %get-tuple-element.10, f32[]{:T(128)} %get-tuple-element.11), channel_id=1, replica_groups=mesh['dp_0'=8,'dp_1'=4,'dp_2'=2,'dp_3'=2,'tensor'=2] {'tensor'}, use_global_device_ids=true, to_apply=%region_7.8 | all-reduce | flops 2 | bytes 16 | tf_op jit(solution)/shard_map/psum | solution.py:56
  269.4 0.0 copy-done.2
  269.4 0.0 copy-done.3
  269.4 0.0 copy-done.4
  269.4 0.6 multiply_add_fusion
  (3 shorter events, 0.1 us)
Async XLA Ops:
  7.2 2.9 %copy-start = (bf16[128,2048]{1,0:T(8,128)(2,1)S(1)}, bf16[128,2048]{1,0:T(8,128)(2,1)}, u32[]{:S(2)}) copy-start(bf16[128,2048]{1,0:T(8,128)(2,1)} %param.11) | copy-start | bytes 1572868
  7.2 129.9 %all-gather.2.cloned.1.call-start = ((), (), s32[]{:S(2)}) async-start(), calls=%async_computation.3 | async-start | bytes 5283840 | tf_op jit(solution)/shard_map/all_gather | solution.py:23
  143.9 28.6 %copy-start.1 = (bf16[128,2048]{1,0:T(8,128)(2,1)S(1)}, bf16[128,2048]{1,0:T(8,128)(2,1)}, u32[]{:S(2)}) copy-start(bf16[128,2048]{1,0:T(8,128)(2,1)} %param.12) | copy-start | bytes 1572868
  172.5 3.4 %copy-start.5 = (f32[8]{0:T(128)S(1)}, f32[8]{0:T(128)}, u32[]{:S(2)}) copy-start(f32[8]{0:T(128)} %param.21) | copy-start | bytes 100
  186.6 82.9 %copy-start.2 = (f32[16,256]{1,0:T(8,128)S(1)}, f32[16,256]{1,0:T(8,128)}, u32[]{:S(2)}) copy-start(f32[16,256]{1,0:T(8,128)} %param.13) | copy-start | bytes 49156
  186.6 82.9 %copy-start.3 = (f32[16,256]{1,0:T(8,128)S(1)}, f32[16,256]{1,0:T(8,128)}, u32[]{:S(2)}) copy-start(f32[16,256]{1,0:T(8,128)} %param.15) | copy-start | bytes 49156
  186.6 82.9 %copy-start.4 = (f32[16,256]{1,0:T(8,128)S(1)}, f32[16,256]{1,0:T(8,128)}, u32[]{:S(2)}) copy-start(f32[16,256]{1,0:T(8,128)} %param.16) | copy-start | bytes 49156
  187.8 35.6 %all-to-all-start.2 = ((f32[64,16,256]{2,1,0:T(8,128)}), f32[64,16,256]{2,1,0:T(8,128)S(1)}, u32[]{:S(2)}, u32[]{:S(2)}) async-start(f32[64,16,256]{2,1,0:T(8,128)} %reduce_sum.57), calls=%async_computation.2 | async-start | bytes 2097152 | tf_op jit(solution)/shard_map/all_to_all | solution.py:51
Sparse Core Ops, SparseCore 0:
  11.6 125.4 all-gather.1
where the time goes:
time: 279 us; the launch traced here: 278 us
  waiting for transfers between devices  149 us (53%)
  blocking collectives  77.4 us (28%)
  between operations  17.4 us (6%)
  matrix products  13 us (5%)
  other arithmetic  8.35 us (3%)
  starting transfers between devices  7.89 us (3%)
  local copies, waits for them, and re-layouts  4.93 us (2%)
    all_gather x1, waiting for transfers between devices, sent_together(): whole = lax.all_gather(both, axis, axis=dim, tiled=True)  124 us
    psum x5, blocking collectives, one_axis_at_a_time(): x = lax.psum(x, axis)  43.9 us
    all_to_all x1, blocking collectives, sent_to_all(): lax.all_to_all(jnp.broadcast_to(x[None], (peers, *x.shape)), axis, 0, 0,...  27.3 us
    all_to_all x1, waiting for transfers between devices, sum_in_two_steps(): return jnp.sum(lax.all_to_all(own, far, 0, 0, tiled=True), axis=0)  25 us
    all_to_all x1, starting transfers between devices, sum_in_two_steps(): return jnp.sum(lax.all_to_all(own, far, 0, 0, tiled=True), axis=0)  7.85 us
    all_to_all x1, blocking collectives, sum_at_owner(): pieces = lax.all_to_all(cut_along(x, dim, peers), axis, 0, 0, tiled=True)  6.16 us
  transfers between devices with their start and end apart: 2, of which 2 were waited for; matrix products, arithmetic and copies ran while one was open for 2% of the time, Pallas kernels for 0%

commit v1 on v0

--- a/solution.py
+++ b/solution.py
@@ -53,7 +53,7 @@
 
 def one_axis_at_a_time(x, axes):
     for axis in axes:
-        x = lax.psum(x, axis)
+        x = jnp.sum(lax.all_gather(x, axis), axis=0)
     return x
 
 

time: 279 us -> 297 us (1.065)
  local copies, waits for them, and re-layouts: 4.93 us -> 21.3 us
  other arithmetic: 8.35 us -> 14.4 us
  blocking collectives: 77.4 us -> 74.3 us
    psum x5 -> x0, blocking collectives: 43.9 us -> none  [one_axis_at_a_time(): x = lax.psum(x, axis)]
    unnamed x0 -> x5, blocking collectives: none -> 40.8 us
    unnamed x12 -> x47, local copies, waits for them, and re-layouts: 0.03 us -> 16.4 us
    reduce_sum x0 -> x10, other arithmetic: none -> 6.01 us  [one_axis_at_a_time(): x = jnp.sum(lax.all_gather(x, axis), axis=0)]
where the time goes in v1:
time: 297 us; the launch traced here: 296 us
  waiting for transfers between devices  148 us (50%)
  blocking collectives  74.3 us (25%)
  local copies, waits for them, and re-layouts  21.3 us (7%)
  between operations  17.4 us (6%)
  other arithmetic  14.4 us (5%)
  matrix products  13 us (4%)
  starting transfers between devices  7.89 us (3%)
    all_gather x1, waiting for transfers between devices, sent_together(): whole = lax.all_gather(both, axis, axis=dim, tiled=True)  124 us
    unnamed x5, blocking collectives  40.8 us
    all_to_all x1, blocking collectives, sent_to_all(): lax.all_to_all(jnp.broadcast_to(x[None], (peers, *x.shape)), axis, 0, 0,...  27.3 us
    all_to_all x1, waiting for transfers between devices, sum_in_two_steps(): return jnp.sum(lax.all_to_all(own, far, 0, 0, tiled=True), axis=0)  23.6 us
    unnamed x47, local copies, waits for them, and re-layouts  16.4 us
    all_to_all x1, starting transfers between devices, sum_in_two_steps(): return jnp.sum(lax.all_to_all(own, far, 0, 0, tiled=True), axis=0)  7.85 us
    all_to_all x1, blocking collectives, sum_at_owner(): pieces = lax.all_to_all(cut_along(x, dim, peers), axis, 0, 0, tiled=True)  6.16 us
    reduce_sum x10, other arithmetic, one_axis_at_a_time(): x = jnp.sum(lax.all_gather(x, axis), axis=0)  6.01 us
  transfers between devices with their start and end apart: 2, of which 2 were waited for; matrix products, arithmetic and copies ran while one was open for 2% of the time, Pallas kernels for 0%

profile of v1, /device:TPU:1, one launch (start us, length us, event | category | flops | bytes accessed | tf_op | source)
XLA Modules:
  0.0 295.9 jit_solution(9022115795669282368)
XLA Ops:
  7.2 0.0 copy-start
  7.2 0.0 all-gather.2.cloned.1.call-start
  7.2 0.8 convert_element_type.37
  8.0 1.4 pad_maximum_fusion
  9.4 0.0 all-gather.2.cloned.1.call-update
  9.4 0.7 exp.13
  10.1 1.0 compare_select_fusion
  11.1 0.1 fusion.17
  11.1 0.1 copy.30
  11.3 0.2 reduce_window_sum.11
  11.5 1.2 fusion.25
  12.7 0.3 fusion.14
  13.0 124.1 %all-gather.2.cloned.1.call-done = bf16[2048,1280]{1,0:T(8,128)(2,1)} async-done(((bf16[16,1280]{1,0:T(8,128)(2,1)}), bf16[2048,1280]{1,0:T(8,128)(2,1)}) %all-gather.2.cloned.1.call-update) | async-done | bytes 5242896 | tf_op jit(solution)/shard_map/all_gather | solution.py:23
  137.1 1.7 convolution_convert_fusion
  138.9 1.0 fusion.9
  139.9 3.7 %fusion.2 = f32[128,2048]{1,0:T(8,128)S(1)} fusion(bf16[128,1024]{0,1:T(8,128)(2,1)S(1)} %bitcast.74, bf16[2048,1280]{1,0:T(8,128)(2,1)} %all-gather.2.cloned.1.call-done), kind=kOutput, calls=%fused_computation.2 | convolution fusion | flops 536870912 | bytes 5505024 | tf_op jit(solution)/shard_map/dot_general | solution.py:114
  143.6 0.2 broadcast_in_dim.16
  143.9 27.3 %all_to_all.16 = f32[2,128,2048]{2,1,0:T(8,128)S(1)} all-to-all(f32[2,128,2048]{2,1,0:T(8,128)S(1)} %broadcast_in_dim.16), channel_id=1, replica_groups=mesh['dp_0'=8,'dp_1'=4,'dp_2'=2,'dp_3'=2,'tensor'=2] {'tensor'}, dimensions={0} | all-to-all | bytes 4194304 | tf_op jit(solution)/shard_map/all_to_all | solution.py:29
  171.2 1.2 reduce_sum.144
  172.5 3.2 %fusion.6 = bf16[128,1024]{1,0:T(8,128)(2,1)S(1)} fusion(bf16[2048,1280]{1,0:T(8,128)(2,1)} %all-gather.2.cloned.1.call-done, f32[128,2048]{1,0:T(8,128)} %reduce_sum.144, bf16[128,2048]{1,0:T(8,128)(2,1)S(1)} %copy-done.1), kind=kOutput, calls=%fused_computation.9 | convolution fusion | flops 537788416 | bytes 6029312 | tf_op jit(solution)/shard_map/dot_general | solution.py:121
  175.7 0.2 copy.33
  175.9 0.4 bitcast_reduce_fusion
  176.3 0.4 convolution_bitcast_fusion
  176.7 1.9 copy.34
  178.6 1.8 copy.35
  180.4 0.0 copy-start.10
  180.4 6.2 %all_to_all.15 = f32[2,64,16,256]{3,2,1,0:T(8,128)S(1)} all-to-all(f32[2,64,16,256]{3,2,1,0:T(8,128)S(1)} %copy.35), channel_id=1, replica_groups=mesh['dp_0'=8,'dp_1'=4,'dp_2'=2,'dp_3'=2,'tensor'=2] {'dp_3'}, dimensions={0} | all-to-all | bytes 4194304 | tf_op jit(solution)/shard_map/all_to_all | solution.py:44
  186.6 1.3 reduce_sum.152
  187.9 7.8 %all-to-all-start.2 = ((f32[64,16,256]{2,1,0:T(8,128)}), f32[64,16,256]{2,1,0:T(8,128)S(1)}, u32[]{:S(2)}, u32[]{:S(2)}) async-start(f32[64,16,256]{2,1,0:T(8,128)} %reduce_sum.152), calls=%async_computation.2 | async-start | bytes 2097152 | tf_op jit(solution)/shard_map/all_to_all | solution.py:51
  195.7 0.6 dynamic-slice
  196.3 2.1 multiply_reduce_fusion
  199.1 0.8 dynamic-update-slice
  199.8 23.6 %all-to-all-done.2 = f32[64,16,256]{2,1,0:T(8,128)S(1)} async-done(((f32[64,16,256]{2,1,0:T(8,128)}), f32[64,16,256]{2,1,0:T(8,128)S(1)}, u32[]{:S(2)}, u32[]{:S(2)}) %all-to-all-start.2) | async-done | bytes 1048608 | tf_op jit(solution)/shard_map/all_to_all | solution.py:51
  223.4 0.1 reduce_sum.153
  223.5 0.6 multiply_reduce_fusion.1
  224.1 1.4 dynamic-update-slice.5
  225.5 0.6 dynamic-slice.1
  226.1 13.6 %all-reduce.10 = (f32[8]{0:T(128)S(1)}, f32[8]{0:T(128)S(1)}) all-reduce(f32[8]{0:T(128)S(1)} %dynamic-update-slice, f32[8]{0:T(128)S(1)} %dynamic-update-slice.5), channel_id=1, replica_groups=mesh['dp_0'=8,'dp_1'=4,'dp_2'=2,'dp_3'=2,'tensor'=2] {'dp_0'}, use_global_device_ids=true, to_apply=%add | all-reduce | flops 16 | bytes 128
  239.7 0.6 reduce_sum.155
  240.3 0.6 reduce_sum.146
  240.9 1.4 dynamic-update-slice.6
  242.3 1.4 dynamic-update-slice.1
  243.7 0.6 dynamic-slice.2
  244.3 6.8 %all-reduce.11 = (f32[4]{0:T(128)S(1)}, f32[4]{0:T(128)S(1)}) all-reduce(f32[4]{0:T(128)S(1)} %dynamic-update-slice.1, f32[4]{0:T(128)S(1)} %dynamic-update-slice.6), channel_id=1, replica_groups=mesh['dp_0'=8,'dp_1'=4,'dp_2'=2,'dp_3'=2,'tensor'=2] {'dp_1'}, use_global_device_ids=true, to_apply=%add.1 | all-reduce | flops 8 | bytes 64
  251.2 0.6 reduce_sum.156
  251.8 0.6 reduce_sum.147
  252.4 1.4 dynamic-update-slice.7
  253.8 1.4 dynamic-update-slice.2
  255.2 0.6 dynamic-slice.3
  255.7 5.3 %all-reduce.14 = (f32[2]{0:T(128)S(1)}, f32[2]{0:T(128)S(1)}) all-reduce(f32[2]{0:T(128)S(1)} %dynamic-update-slice.2, f32[2]{0:T(128)S(1)} %dynamic-update-slice.7), channel_id=1, replica_groups=mesh['dp_0'=8,'dp_1'=4,'dp_2'=2,'dp_3'=2,'tensor'=2] {'dp_2'}, use_global_device_ids=true, to_apply=%add.2 | all-reduce | flops 4 | bytes 32
  261.0 0.6 reduce_sum.157
  261.6 0.6 reduce_sum.148
  262.2 1.4 dynamic-update-slice.8
  263.6 1.4 dynamic-update-slice.3
  265.0 0.6 dynamic-slice.4
  265.6 11.3 %all-reduce.13 = (f32[2]{0:T(128)S(1)}, f32[2]{0:T(128)S(1)}) all-reduce(f32[2]{0:T(128)S(1)} %dynamic-update-slice.3, f32[2]{0:T(128)S(1)} %dynamic-update-slice.8), channel_id=1, replica_groups=mesh['dp_0'=8,'dp_1'=4,'dp_2'=2,'dp_3'=2,'tensor'=2] {'dp_3'}, use_global_device_ids=true, to_apply=%add.3 | all-reduce | flops 4 | bytes 32
  276.9 0.6 reduce_sum.158
  277.5 0.6 reduce_sum.149
  278.1 1.4 dynamic-update-slice.9
  279.5 1.4 dynamic-update-slice.4
  280.9 3.8 %all-reduce.12 = (f32[2]{0:T(128)S(1)}, f32[2]{0:T(128)S(1)}) all-reduce(f32[2]{0:T(128)S(1)} %dynamic-update-slice.4, f32[2]{0:T(128)S(1)} %dynamic-update-slice.9), channel_id=1, replica_groups=mesh['dp_0'=8,'dp_1'=4,'dp_2'=2,'dp_3'=2,'tensor'=2] {'tensor'}, use_global_device_ids=true, to_apply=%add.4 | all-reduce | flops 4 | bytes 32
  284.7 0.6 reduce_sum.159
  286.0 0.6 reduce_sum.150
  287.3 0.6 multiply_add_fusion
  (33 shorter events, 0.2 us)
Async XLA Ops:
  7.2 2.9 copy-start
  7.2 129.9 %all-gather.2.cloned.1.call-start = ((), (), s32[]{:S(2)}) async-start(), calls=%async_computation.3 | async-start | bytes 5283840 | tf_op jit(solution)/shard_map/all_gather | solution.py:23
  143.9 28.6 %copy-start.1 = (bf16[128,2048]{1,0:T(8,128)(2,1)S(1)}, bf16[128,2048]{1,0:T(8,128)(2,1)}, u32[]{:S(2)}) copy-start(bf16[128,2048]{1,0:T(8,128)(2,1)} %param.12) | copy-start | bytes 1572868
  172.5 3.4 %copy-start.5 = (f32[8]{0:T(128)S(1)}, f32[8]{0:T(128)}, u32[]{:S(2)}) copy-start(f32[8]{0:T(128)} %param.21) | copy-start | bytes 100
  180.4 15.3 %copy-start.10 = (u32[256]{0:T(256)S(1)}, u32[256]{0:T(256)}, u32[]{:S(2)}) copy-start(u32[256]{0:T(256)} %constant.46) | copy-start | bytes 3076
  186.6 39.0 %copy-start.9 = (u32[256]{0:T(256)S(1)}, u32[256]{0:T(256)}, u32[]{:S(2)}) copy-start(u32[256]{0:T(256)} %constant.51) | copy-start | bytes 3076
  186.6 57.2 %copy-start.8 = (u32[256]{0:T(256)S(1)}, u32[256]{0:T(256)}, u32[]{:S(2)}) copy-start(u32[256]{0:T(256)} %constant.56) | copy-start | bytes 3076
  186.6 68.6 %copy-start.7 = (u32[256]{0:T(256)S(1)}, u32[256]{0:T(256)}, u32[]{:S(2)}) copy-start(u32[256]{0:T(256)} %constant.61) | copy-start | bytes 3076
  186.6 78.5 %copy-start.6 = (u32[256]{0:T(256)S(1)}, u32[256]{0:T(256)}, u32[]{:S(2)}) copy-start(u32[256]{0:T(256)} %constant.66) | copy-start | bytes 3076
  186.6 100.7 %copy-start.2 = (f32[16,256]{1,0:T(8,128)S(1)}, f32[16,256]{1,0:T(8,128)}, u32[]{:S(2)}) copy-start(f32[16,256]{1,0:T(8,128)} %param.13) | copy-start | bytes 49156
  186.6 100.7 %copy-start.3 = (f32[16,256]{1,0:T(8,128)S(1)}, f32[16,256]{1,0:T(8,128)}, u32[]{:S(2)}) copy-start(f32[16,256]{1,0:T(8,128)} %param.15) | copy-start | bytes 49156
  186.6 100.7 %copy-start.4 = (f32[16,256]{1,0:T(8,128)S(1)}, f32[16,256]{1,0:T(8,128)}, u32[]{:S(2)}) copy-start(f32[16,256]{1,0:T(8,128)} %param.16) | copy-start | bytes 49156
  187.9 35.6 %all-to-all-start.2 = ((f32[64,16,256]{2,1,0:T(8,128)}), f32[64,16,256]{2,1,0:T(8,128)S(1)}, u32[]{:S(2)}, u32[]{:S(2)}) async-start(f32[64,16,256]{2,1,0:T(8,128)} %reduce_sum.152), calls=%async_computation.2 | async-start | bytes 2097152 | tf_op jit(solution)/shard_map/all_to_all | solution.py:51
Sparse Core Ops, SparseCore 0:
  11.6 125.4 all-gather.1
